TPU v7x, 32 devices: a whole 2x2x4 slice. The times are simulated.
32 devices in a mesh: groups: 2 (over y), seq: 4 (over z), beam: 4 (over x, core).
Axes of the slice: x: 2, y: 2, z: 4, core: 2. Of those that a mesh axis runs over, the one named last changes fastest.
Arguments:
- prompt_values: bfloat16 [2048, 8192], P(('groups', 'seq'), 'beam'), parts along dimension 0, may hold values from -6 to 6
- prompt_keys: bfloat16 [2048, 128], P(('groups', 'seq')), parts along dimension 0, may hold values from -0.31445312 to 0.31445312
- prompt_queries: bfloat16 [2048, 128], P(('groups', 'seq')), parts along dimension 0, may hold values from -0.31445312 to 0.31445312
- logarithm_state_decay: float32 [2048, 128], P(('groups', 'seq'), 'beam'), parts along dimension 0, may hold values from -1 to 0
- step_values: bfloat16 [8, 4, 8192], P('groups', 'beam', 'seq'), parts along dimension 0, may hold values from -6 to 6
- step_keys: bfloat16 [8, 4, 128], P('groups', 'beam'), parts along dimension 0, may hold values from -6 to 6
- step_queries: bfloat16 [8, 4, 128], P('groups', 'beam'), parts along dimension 0, may hold values from -0.31445312 to 0.31445312
- step_decay: float32 [8, 4, 128], P('groups', 'beam', 'seq'), parts along dimension 0, may hold values from -0.6 to -0.02
- step_logprob: float32 [8, 4], P('groups', 'beam'), parts along dimension 0, may hold values from -6 to -0.05
- parents: int32 [8, 4], P('groups', 'beam'), parts along dimension 0, may hold values from 0 to 3
- finished: int32 [8, 4], P('groups', 'beam'), parts along dimension 0, may hold values 0 or 1
- lengths: int32 [8], P(('groups', 'beam')), parts along dimension 0, may hold values from 1 to 59
- init_score: float32 [8], P(('groups', 'beam')), parts along dimension 0, may hold values from -20 to -2
Outputs:
- prompt_output: bfloat16 [2048, 8192], P(('groups', 'seq'), 'beam'), parts along dimension 0
- step_output: bfloat16 [8, 4, 8192], P('groups', 'beam', 'seq'), parts along dimension 0
- ranked: float32 [8, 4], P('groups', 'beam'), parts along dimension 0
- beam_states: float32 [8, 8192, 128], P(('groups', 'beam'), 'seq'), parts along dimension 0
There are 2 independent parts, one for each index of `groups`. A program takes and returns all parts, laid end to end along the dimension named above; each array names one. Nothing has to cross between parts.
All inputs are finite; a program needn't handle non-finite values. No bound on the sum of `finished` on one device may be relied on, other than what follows from the above.
Results may differ from a plain program's by a relative error of at most 0.0056.
Values sent between devices are 32-bit elements; how exact they have to be, the bound alone decides.
No kernel may reach another device: no remote copies, remote signals or barrier semaphores. Data moves between devices by JAX's collectives and lax.ppermute only.
A program may use at most 64 MiB of HBM per device.

v0:
```python
import jax
import jax.numpy as jnp
from jax import lax
from jax.sharding import PartitionSpec as P

P_SIZE = 64
N = 128
STEPS = 4
SPAN = 256


def on_device(
    prompt_values,
    prompt_keys,
    prompt_queries,
    logarithm_state_decay,
    step_values,
    step_keys,
    step_queries,
    step_decay,
    step_logprob,
    parents,
    finished,
    lengths,
    init_score,
):
    token_rows = prompt_values.shape[0]
    head_count = logarithm_state_decay.shape[1]
    block_count = token_rows // SPAN
    values_blocks = prompt_values.reshape(block_count, SPAN, head_count, P_SIZE)
    keys_blocks = prompt_keys.reshape(block_count, SPAN, N)
    query_blocks = prompt_queries.reshape(block_count, SPAN, N)
    decay_sums = jnp.cumsum(logarithm_state_decay.reshape(block_count, SPAN, head_count), axis=1)
    lower = jnp.tril(jnp.ones((SPAN, SPAN), dtype=bool))

    def within(item):
        values_one, keys_one, query_one, sums_one = item
        scores = jnp.dot(query_one, keys_one.T, preferred_element_type=jnp.float32)
        spread = jnp.where(lower[:, :, None], sums_one[:, None, :] - sums_one[None, :, :], -jnp.inf)
        weights = (scores[:, :, None] * jnp.exp(spread)).astype(jnp.bfloat16)
        return jnp.einsum("ijh,jhp->ihp", weights, values_one, preferred_element_type=jnp.float32)

    inner_out = lax.map(within, (values_blocks, keys_blocks, query_blocks, decay_sums))
    tail_decay = jnp.exp(decay_sums[:, -1:, :] - decay_sums)
    scaled = (values_blocks * tail_decay[:, :, :, None]).astype(jnp.bfloat16)
    block_states = jnp.einsum(
        "kjhp,kjn->khpn", scaled, keys_blocks, preferred_element_type=jnp.float32
    )
    block_decay = jnp.exp(decay_sums[:, -1, :])

    def advance(carry, item):
        state_now, current_shrink_factor = carry
        single_token_decay, state_one = item
        return (
            (
                single_token_decay[:, None, None] * state_now + state_one,
                current_shrink_factor * single_token_decay,
            ),
            (state_now, current_shrink_factor),
        )

    zero_state = jnp.zeros((head_count, P_SIZE, N), jnp.float32)
    unit_decay = jnp.ones((head_count,), jnp.float32)
    (segment_finish, total_decay), (before, prior) = lax.scan(
        advance, (zero_state, unit_decay), (block_decay, block_states)
    )
    seq_index = lax.axis_index("seq")
    all_decays, all_states = (
        lax.all_gather(total_decay[None], "seq", axis=0, tiled=True),
        lax.all_gather(segment_finish[None], "seq", axis=0, tiled=True),
    )
    piece_ids = jnp.arange(all_decays.shape[0], dtype=jnp.int32)

    def collect(carry, item):
        running, mine = carry
        decay_one, state_one, piece_id = item
        mine = jnp.where(piece_id == seq_index, running, mine)
        running = decay_one[:, None, None] * running + state_one
        return ((running, mine), None)

    (full_block, arriving_input), unused = lax.scan(
        collect, (zero_state, zero_state), (all_decays, all_states, piece_ids)
    )
    starts = prior[:, :, None, None] * arriving_input[None] + before
    carried = (
        jnp.einsum(
            "kin,khpn->kihp",
            query_blocks,
            starts.astype(jnp.bfloat16),
            preferred_element_type=jnp.float32,
        )
        * jnp.exp(decay_sums)[:, :, :, None]
    )
    prompt_output = (
        (inner_out + carried).astype(jnp.bfloat16).reshape(token_rows, head_count * P_SIZE)
    )
    group_heads = step_values.shape[2] // P_SIZE
    first_head = seq_index * group_heads
    every_head = lax.all_gather(full_block, "beam", axis=0, tiled=True)
    own_heads = lax.dynamic_slice_in_dim(every_head, first_head, group_heads, 0)
    state_now = own_heads
    score_now = init_score
    length_now = lengths.astype(jnp.float32)
    step_list = []
    ranked_list = []
    for step_index in range(STEPS):
        parent_now = parents[step_index, 0]
        pieces = (
            lax.all_gather(state_now[None], "beam", axis=0, tiled=True),
            lax.all_gather(score_now, "beam", axis=0, tiled=True),
            lax.all_gather(length_now, "beam", axis=0, tiled=True),
        )
        slot_ids = jnp.arange(pieces[0].shape[0], dtype=jnp.int32)
        picked = (slot_ids == parent_now).astype(jnp.float32)
        state_part = jnp.sum(picked[:, None, None, None] * pieces[0], axis=0, keepdims=True)
        score_part = jnp.sum(picked * pieces[1]).reshape(1)
        length_part = jnp.sum(picked * pieces[2]).reshape(1)
        done = finished[step_index, 0] == 1
        live = (1 - finished[step_index]).astype(jnp.float32)
        values_now = step_values[step_index, 0].astype(jnp.float32).reshape(group_heads, P_SIZE)
        keys_now = step_keys[step_index, 0].astype(jnp.float32)
        updated = (
            jnp.exp(step_decay[step_index, 0])[:, None, None] * state_part[0]
            + values_now[:, :, None] * keys_now[None, None, :]
        )
        state_now = jnp.where(done, state_part[0], updated)
        output_now = jnp.einsum(
            "hpn,n->hp",
            state_now.astype(jnp.bfloat16),
            step_queries[step_index, 0],
            preferred_element_type=jnp.float32,
        )
        output_now = jnp.where(done, jnp.float32(0.0), output_now)
        step_list.append(output_now.reshape(1, group_heads * P_SIZE).astype(jnp.bfloat16))
        score_now = score_part + live * step_logprob[step_index]
        length_now = length_part + live
        normed = score_now / ((5.0 + length_now) / 6.0) ** 0.6
        best = lax.pmax(normed, "beam")
        ranked_list.append(normed - best)
    step_output = jnp.stack(step_list)
    ranked = jnp.stack(ranked_list)
    beam_states = state_now.reshape(1, group_heads * P_SIZE, N)
    return (prompt_output, step_output, ranked, beam_states)


def solution(mesh):
    return jax.shard_map(
        on_device,
        mesh=mesh,
        in_specs=(
            P(("groups", "seq"), "beam"),
            P(("groups", "seq"), None),
            P(("groups", "seq"), None),
            P(("groups", "seq"), "beam"),
            P("groups", "beam", "seq"),
            P("groups", "beam", None),
            P("groups", "beam", None),
            P("groups", "beam", "seq"),
            P("groups", "beam"),
            P("groups", "beam"),
            P("groups", "beam"),
            P(("groups", "beam")),
            P(("groups", "beam")),
        ),
        out_specs=(
            P(("groups", "seq"), "beam"),
            P("groups", "beam", "seq"),
            P("groups", "beam"),
            P(("groups", "beam"), "seq", None),
        ),
        check_vma=False,
    )
```

profile of v0, /device:TPU:0, one launch (start us, length us, event | category | flops | bytes accessed | tf_op | source)
XLA Modules:
  0.0 360.7 jit_solution(6325629616704435772)
XLA Ops:
  12.3 12.6 %all-gather = f32[4,1,32]{2,1,0:T(1,128)S(1)} all-gather(f32[1,1,32]{2,1,0:T(1,128)S(1)} %get-tuple-element.163), channel_id=2, replica_groups=mesh['groups'=2,'seq'=4,'beam'=4] {'seq'}, dimensions={0}, use_global_device_ids=true | all-gather | bytes 640 | tf_op jit(solution)/shard_map/all_gather | solution.py:69
  25.0 70.9 %all-gather.18.cloned.1.call-done = f32[128,64,128]{2,1,0:T(8,128)} async-done(((f32[32,64,128]{2,1,0:T(8,128)}), f32[128,64,128]{2,1,0:T(8,128)}) %all-gather.18.cloned.1.call-update) | async-done | bytes 4194320 | tf_op jit(solution)/shard_map/all_gather | solution.py:70
  95.9 11.8 %while.3 = (s32[]{:T(128)}, f32[32,64,128]{2,1,0:T(8,128)S(1)}, bf16[32,64,128]{2,1,0:T(8,128)(2,1)S(1)}, f32[4,32]{1,0:T(4,128)S(1)}, f32[4,32,64,128]{3,2,1,0:...) while((s32[]{:T(128)}, f32[32,64,128]{2,1,0:T(8,128)S(1)}, ...), condition=%wide.region_3.4_spmd.clone, body=%wide.region_2.3_spmd.clone.sunk | while | flops 1572868 | bytes 5243406 | solution.py:81
  108.7 33.0 %all-gather.10.cloned.1.call-done = f32[128,64,128]{2,1,0:T(8,128)} async-done(((f32[32,64,128]{2,1,0:T(8,128)}), f32[128,64,128]{2,1,0:T(8,128)}) %all-gather.10.cloned.1.call-update) | async-done | bytes 4194320 | tf_op jit(solution)/shard_map/all_gather | solution.py:99
  141.8 2.3 constant_dynamic-slice_fusion
  146.9 31.8 %all-gather.20.cloned.1.call-done = f32[128,64,128]{2,1,0:T(8,128)} async-done(((f32[32,64,128]{2,1,0:T(8,128)}), f32[128,64,128]{2,1,0:T(8,128)}) %all-gather.20.cloned.1.call-update) | async-done | bytes 4194320 | tf_op jit(solution)/shard_map/all_gather | solution.py:109
  178.7 2.9 multiply_reduce_fusion.3
  184.4 33.2 %all-gather.12.cloned.1.call-done = f32[4,32,64,128]{3,2,1,0:T(8,128)} async-done(((f32[1,32,64,128]{3,2,1,0:T(8,128)}), f32[4,32,64,128]{3,2,1,0:T(8,128)}) %all-gather.12.cloned.1.call-update) | async-done | bytes 4194320 | tf_op jit(solution)/shard_map/all_gather | solution.py:109
  217.6 2.9 multiply_reduce_fusion.2
  224.2 33.2 %all-gather.14.cloned.1.call-done = f32[4,32,64,128]{3,2,1,0:T(8,128)} async-done(((f32[1,32,64,128]{3,2,1,0:T(8,128)}), f32[4,32,64,128]{3,2,1,0:T(8,128)}) %all-gather.14.cloned.1.call-update) | async-done | bytes 4194320 | tf_op jit(solution)/shard_map/all_gather | solution.py:109
  257.4 2.9 multiply_reduce_fusion.1
  266.1 5.9 %all-reduce.11 = (f32[4]{0:T(128)S(1)}, f32[4]{0:T(128)S(1)}) all-reduce(f32[4]{0:T(128)S(1)} %dynamic-update-slice, f32[4]{0:T(128)S(1)} %convert_dynamic-update-slice_fusion), channel_id=1, replica_groups=mesh['groups'=2,'seq'=4,'beam'=4] {'beam'}, use_global_device_ids=true, to_apply=%add | all-reduce | flops 8 | bytes 64
  276.5 1.7 fusion.50
  281.1 6.5 %all-reduce.10 = (f32[4]{0:T(128)S(1)}, f32[4]{0:T(128)S(1)}) all-reduce(f32[4]{0:T(128)S(1)} %dynamic-update-slice.2, f32[4]{0:T(128)S(1)} %dynamic-update-slice.3), channel_id=1, replica_groups=mesh['groups'=2,'seq'=4,'beam'=4] {'beam'}, use_global_device_ids=true, to_apply=%add.2 | all-reduce | flops 8 | bytes 64
  292.6 1.7 fusion.48
  297.1 6.1 %all-reduce.9 = (f32[4]{0:T(128)S(1)}, f32[4]{0:T(128)S(1)}) all-reduce(f32[4]{0:T(128)S(1)} %dynamic-update-slice.4, f32[4]{0:T(128)S(1)} %dynamic-update-slice.5), channel_id=1, replica_groups=mesh['groups'=2,'seq'=4,'beam'=4] {'beam'}, use_global_device_ids=true, to_apply=%add.4 | all-reduce | flops 8 | bytes 64
  308.2 1.9 fusion.46
  312.8 6.1 %all-reduce.8 = (f32[4]{0:T(128)S(1)}, f32[4]{0:T(128)S(1)}) all-reduce(f32[4]{0:T(128)S(1)} %dynamic-update-slice.6, f32[4]{0:T(128)S(1)} %dynamic-update-slice.7), channel_id=1, replica_groups=mesh['groups'=2,'seq'=4,'beam'=4] {'beam'}, use_global_device_ids=true, to_apply=%add.6 | all-reduce | flops 8 | bytes 64
  324.2 7.0 %all-reduce.12 = (f32[1]{0:T(128)}, f32[1]{0:T(128)}, f32[1]{0:T(128)}, f32[1]{0:T(128)}) all-reduce(f32[1]{0:T(128)S(6)} %div.31, f32[1]{0:T(128)} %get-tuple-element.186, f32[1]{0:T(128)} %get-tuple-element.190, f32[1]{0:T(128)} %get-tuple-element.194), channel_id=1, replica_groups=mesh['groups'=2,'seq'=4,'beam'=4] {'beam'}, use_global_device_ids=true, to_apply=%region_19.20 | all-reduce | flops 4 | bytes 32 | tf_op jit(solution)/shard_map/pmax | solution.py:138
  338.7 3.7 %fusion.7 = bf16[256,32,64]{0,2,1:T(8,128)(2,1)} fusion(f32[32,64,256]{2,1,0:T(8,128)S(1)} %fusion.13, bf16[256,32,64]{0,2,1:T(8,128)(2,1)S(1)} %bitcast.193, f32[256,32]{0,1:T(8,128)S(1)} %copy.48, f32[256,256]{1,0:T(8,128)S(1)} %fusion.51, pred[256,256]{1,0:T(8,128)(4,1)S(1)} %iota_compare_fusion, f32[256,32]{0,1:T(8,128)S(1)} %copy.53), kind=kOutput, calls=%fused_computation.16 | convolution fusion | flops 278396928 | bytes 4587520 | tf_op jit(solution)/shard_map/while/body/eval_jaxpr/ijh,jhp->ihp/dot_general | solution.py:41
  342.4 2.4 copy.54
  345.4 1.8 fusion.16
  348.0 2.9 multiply_reduce_fusion
  351.6 1.6 bitcast_select_fusion
  (140 shorter events, 53.5 us)
Async XLA Ops:
  7.2 330.8 %copy-start = (bf16[256,128]{1,0:T(8,128)(2,1)S(1)}, bf16[256,128]{1,0:T(8,128)(2,1)}, u32[]{:S(2)}) copy-start(bf16[256,128]{1,0:T(8,128)(2,1)} %param.17) | copy-start | bytes 196612
  7.2 3.6 %copy-start.5 = (bf16[256,128]{1,0:T(8,128)(2,1)S(1)}, bf16[256,128]{1,0:T(8,128)(2,1)}, u32[]{:S(2)}) copy-start(bf16[256,128]{1,0:T(8,128)(2,1)} %param.16) | copy-start | bytes 196612
  7.2 88.7 %all-gather.18.cloned.1.call-start = ((), (), s32[]{:S(2)}) async-start(), calls=%async_computation.4 | async-start | bytes 5242880 | tf_op jit(solution)/shard_map/all_gather | solution.py:70
  12.3 129.5 %all-gather.10.cloned.1.call-start = ((), (), s32[]{:S(2)}) async-start(), calls=%async_computation | async-start | bytes 5242880 | tf_op jit(solution)/shard_map/all_gather | solution.py:99
  107.7 1.0 copy-start.1
  107.7 36.5 %copy-start.6 = (bf16[4,1,2048]{2,0,1:T(4,128)(2,1)S(1)}, bf16[4,1,2048]{2,0,1:T(4,128)(2,1)}, u32[]{:S(2)}) copy-start(bf16[4,1,2048]{2,0,1:T(4,128)(2,1)} %param.19) | copy-start | bytes 49156
  107.7 36.6 %copy-start.7 = (s32[4,1]{0,1:T(1,128)S(1)}, s32[4,1]{0,1:T(1,128)}, u32[]{:S(2)}) copy-start(s32[4,1]{0,1:T(1,128)} %param.25) | copy-start | bytes 52
  107.7 37.9 %copy-start.8 = (s32[4,1]{0,1:T(1,128)S(1)}, s32[4,1]{0,1:T(1,128)}, u32[]{:S(2)}) copy-start(s32[4,1]{0,1:T(1,128)} %param.24) | copy-start | bytes 52
  107.7 39.2 %copy-start.11 = (f32[4,1,32]{2,1,0:T(1,128)S(1)}, f32[4,1,32]{2,1,0:T(1,128)}, u32[]{:S(2)}) copy-start(f32[4,1,32]{2,1,0:T(1,128)} %param.22) | copy-start | bytes 1540
  107.7 39.2 %copy-start.10 = (bf16[4,1,128]{2,0,1:T(4,128)(2,1)S(1)}, bf16[4,1,128]{2,0,1:T(4,128)(2,1)}, u32[]{:S(2)}) copy-start(bf16[4,1,128]{2,0,1:T(4,128)(2,1)} %param.20) | copy-start | bytes 3076
  108.7 70.0 %all-gather.20.cloned.1.call-start = ((), (), s32[]{:S(2)}) async-start(), calls=%async_computation.5 | async-start | bytes 5242880 | tf_op jit(solution)/shard_map/all_gather | solution.py:109
  144.1 73.5 %all-gather.12.cloned.1.call-start = ((), (), s32[]{:S(2)}) async-start(), calls=%async_computation.1 | async-start | bytes 5242880 | tf_op jit(solution)/shard_map/all_gather | solution.py:109
  183.0 74.5 %all-gather.14.cloned.1.call-start = ((), (), s32[]{:S(2)}) async-start(), calls=%async_computation.2 | async-start | bytes 5242880 | tf_op jit(solution)/shard_map/all_gather | solution.py:109
  220.5 1.0 copy-start.2
  222.8 125.2 %all-gather.16.cloned.1.call-start = ((), (), s32[]{:S(2)}) async-start(), calls=%async_computation.3 | async-start | bytes 5242880 | tf_op jit(solution)/shard_map/all_gather | solution.py:109
  224.2 39.8 %copy-start.13 = (u32[32]{0:T(128)S(1)}, u32[32]{0:T(128)}, u32[]{:S(2)}) copy-start(u32[32]{0:T(128)} %constant.105) | copy-start | bytes 388
  224.2 51.6 %copy-start.9 = (f32[4,1]{0,1:T(1,128)S(1)}, f32[4,1]{0,1:T(1,128)}, u32[]{:S(2)}) copy-start(f32[4,1]{0,1:T(1,128)} %param.23) | copy-start | bytes 52
  260.3 1.0 copy-start.3
  338.7 6.1 %copy-start.12 = (bf16[4,1,128]{2,0,1:T(4,128)(2,1)S(1)}, bf16[4,1,128]{2,0,1:T(4,128)(2,1)}, u32[]{:S(2)}) copy-start(bf16[4,1,128]{2,0,1:T(4,128)(2,1)} %param.21) | copy-start | bytes 3076
  342.4 5.0 %copy-start.4 = (f32[32,64,128]{2,1,0:T(8,128)S(1)}, f32[32,64,128]{2,1,0:T(8,128)}, u32[]{:S(2)}) copy-start(f32[32,64,128]{2,1,0:T(8,128)} %copy-done.3) | copy-start | bytes 3145732
Sparse Core Ops, SparseCore 0:
  12.4 83.4 all-gather.17
  108.8 32.9 all-gather.9
  144.2 34.4 all-gather.19
  183.1 34.4 all-gather.11
  222.9 34.4 all-gather.13
  262.9 34.5 all-gather.15
where the time goes:
time: 362 us; the launch traced here: 361 us
  waiting for transfers between devices  202 us (56%)
  other arithmetic  47.2 us (13%)
  blocking collectives  44.2 us (12%)
  between operations  29.5 us (8%)
  local copies, waits for them, and re-layouts  25.3 us (7%)
  matrix products  9.29 us (3%)
    all_gather x4, waiting for transfers between devices, on_device(): lax.all_gather(state_now[None], 'beam', axis=0, tiled=True)  98.2 us
    all_gather x1, waiting for transfers between devices, on_device(): lax.all_gather(segment_finish[None], 'seq', axis=0, tiled=True)  70.9 us
    all_gather x1, waiting for transfers between devices, on_device(): every_head = lax.all_gather(full_block, 'beam', axis=0, tiled=True)  33 us
    unnamed x4, blocking collectives  24.6 us
    unnamed x46, local copies, waits for them, and re-layouts  16.5 us
    all_gather x1, blocking collectives, on_device(): lax.all_gather(total_decay[None], 'seq', axis=0, tiled=True)  12.6 us
    reduce_sum x4, other arithmetic, on_device(): jnp.sum(picked[:, None, None, None] * pieces[0], axis=0, keepdims=True)  11.5 us
  transfers between devices with their start and end apart: 6, of which 5 were waited for; matrix products, arithmetic and copies ran while one was open for 12% of the time, Pallas kernels for 0%

commit v1 on v0

--- a/solution.py
+++ b/solution.py
@@ -96,7 +96,13 @@
     )
     group_heads = step_values.shape[2] // P_SIZE
     first_head = seq_index * group_heads
-    every_head = lax.all_gather(full_block, "beam", axis=0, tiled=True)
+    peers = lax.axis_size("beam")
+    held, parts = (full_block, [full_block])
+    for _ in range(peers - 1):
+        held = lax.ppermute(held, "beam", [(i, (i + 1) % peers) for i in range(peers)])
+        parts.insert(0, held)
+    merged = jnp.concatenate(parts, axis=0)
+    every_head = jnp.roll(merged, (lax.axis_index("beam") + 1) * full_block.shape[0], axis=0)
     own_heads = lax.dynamic_slice_in_dim(every_head, first_head, group_heads, 0)
     state_now = own_heads
     score_now = init_score

time: 362 us -> 378 us (1.044)
  waiting for transfers between devices: 202 us -> 211 us
  local copies, waits for them, and re-layouts: 25.3 us -> 31 us
    ppermute x0 -> x3, waiting for transfers between devices: none -> 43.1 us  [on_device(): lax.ppermute(held, 'beam', [(i, (i + 1) % peers) for i in range(peers)])]
    all_gather x1 -> x0, waiting for transfers between devices: 33 us -> none  [on_device(): every_head = lax.all_gather(full_block, 'beam', axis=0, tiled=True)]
    unnamed x46 -> x53, local copies, waits for them, and re-layouts: 16.5 us -> 23.4 us
  transfers between devices with their start and end apart: 6 -> 8, of which waited for: 5 -> 7; matrix products, arithmetic and copies ran while one was open for 12% -> 12% of each run, Pallas kernels for 0% -> 0%
where the time goes in v1:
time: 378 us; the launch traced here: 377 us
  waiting for transfers between devices  211 us (56%)
  other arithmetic  47.2 us (12%)
  blocking collectives  44.2 us (12%)
  local copies, waits for them, and re-layouts  31 us (8%)
  between operations  29.3 us (8%)
  matrix products  11.4 us (3%)
    all_gather x4, waiting for transfers between devices, on_device(): lax.all_gather(state_now[None], 'beam', axis=0, tiled=True)  96.6 us
    all_gather x1, waiting for transfers between devices, on_device(): lax.all_gather(segment_finish[None], 'seq', axis=0, tiled=True)  70.9 us
    ppermute x3, waiting for transfers between devices, on_device(): lax.ppermute(held, 'beam', [(i, (i + 1) % peers) for i in range(peers)])  43.1 us
    unnamed x4, blocking collectives  24.6 us
    unnamed x53, local copies, waits for them, and re-layouts  23.4 us
    all_gather x1, blocking collectives, on_device(): lax.all_gather(total_decay[None], 'seq', axis=0, tiled=True)  12.6 us
    reduce_sum x4, other arithmetic, on_device(): jnp.sum(picked[:, None, None, None] * pieces[0], axis=0, keepdims=True)  11.5 us
  transfers between devices with their start and end apart: 8, of which 7 were waited for; matrix products, arithmetic and copies ran while one was open for 12% of the time, Pallas kernels for 0%

profile of v1, /device:TPU:0, one launch (start us, length us, event | category | flops | bytes accessed | tf_op | source)
XLA Modules:
  0.0 376.8 jit_solution(14266334318178534968)
XLA Ops:
  10.8 2.2 convolution_add_fusion
  13.1 12.6 %all-gather = f32[4,1,32]{2,1,0:T(1,128)S(1)} all-gather(f32[1,1,32]{2,1,0:T(1,128)S(1)} %get-tuple-element.163), channel_id=2, replica_groups=mesh['groups'=2,'seq'=4,'beam'=4] {'seq'}, dimensions={0}, use_global_device_ids=true | all-gather | bytes 640 | tf_op jit(solution)/shard_map/all_gather | solution.py:69
  25.8 70.9 %all-gather.15.cloned.1.call-done = f32[128,64,128]{2,1,0:T(8,128)} async-done(((f32[32,64,128]{2,1,0:T(8,128)}), f32[128,64,128]{2,1,0:T(8,128)}) %all-gather.15.cloned.1.call-update) | async-done | bytes 4194320 | tf_op jit(solution)/shard_map/all_gather | solution.py:70
  96.7 11.8 %while.3 = (s32[]{:T(128)}, f32[32,64,128]{2,1,0:T(8,128)S(1)}, bf16[32,64,128]{2,1,0:T(8,128)(2,1)S(1)}, f32[4,32]{1,0:T(4,128)S(1)}, f32[4,32,64,128]{3,2,1,0:...) while((s32[]{:T(128)}, f32[32,64,128]{2,1,0:T(8,128)S(1)}, ...), condition=%wide.region_3.4_spmd.clone, body=%wide.region_2.3_spmd.clone.sunk | while | flops 1572868 | bytes 5243406 | solution.py:81
  108.5 14.2 %collective-permute-done = f32[32,64,128]{2,1,0:T(8,128)S(1)} collective-permute-done((f32[32,64,128]{2,1,0:T(8,128)S(1)}, f32[32,64,128]{2,1,0:T(8,128)S(1)}, u32[]{:S(2)}, u32[]{:S(2)}) %collective-permute-start) | collective-permute-done | bytes 1048608 | tf_op jit(solution)/shard_map/ppermute | solution.py:102
  123.7 14.3 %collective-permute-done.1 = f32[32,64,128]{2,1,0:T(8,128)} collective-permute-done((f32[32,64,128]{2,1,0:T(8,128)S(1)}, f32[32,64,128]{2,1,0:T(8,128)}, u32[]{:S(2)}, u32[]{:S(2)}) %collective-permute-start.1) | collective-permute-done | bytes 1048608 | tf_op jit(solution)/shard_map/ppermute | solution.py:102
  138.0 14.5 %collective-permute-done.2 = f32[32,64,128]{2,1,0:T(8,128)} collective-permute-done((f32[32,64,128]{2,1,0:T(8,128)}, f32[32,64,128]{2,1,0:T(8,128)}, u32[]{:S(2)}, u32[]{:S(2)}) %collective-permute-start.2) | collective-permute-done | bytes 1048608 | tf_op jit(solution)/shard_map/ppermute | solution.py:102
  163.6 30.2 %all-gather.17.cloned.1.call-done = f32[128,64,128]{2,1,0:T(8,128)} async-done(((f32[32,64,128]{2,1,0:T(8,128)}), f32[128,64,128]{2,1,0:T(8,128)}) %all-gather.17.cloned.1.call-update) | async-done | bytes 4194320 | tf_op jit(solution)/shard_map/all_gather | solution.py:115
  193.8 2.9 multiply_reduce_fusion.3
  199.5 33.2 %all-gather.9.cloned.1.call-done = f32[4,32,64,128]{3,2,1,0:T(8,128)} async-done(((f32[1,32,64,128]{3,2,1,0:T(8,128)}), f32[4,32,64,128]{3,2,1,0:T(8,128)}) %all-gather.9.cloned.1.call-update) | async-done | bytes 4194320 | tf_op jit(solution)/shard_map/all_gather | solution.py:115
  232.7 2.9 multiply_reduce_fusion.2
  239.3 33.2 %all-gather.11.cloned.1.call-done = f32[4,32,64,128]{3,2,1,0:T(8,128)} async-done(((f32[1,32,64,128]{3,2,1,0:T(8,128)}), f32[4,32,64,128]{3,2,1,0:T(8,128)}) %all-gather.11.cloned.1.call-update) | async-done | bytes 4194320 | tf_op jit(solution)/shard_map/all_gather | solution.py:115
  272.5 2.9 multiply_reduce_fusion.1
  281.3 5.9 %all-reduce.11 = (f32[4]{0:T(128)S(1)}, f32[4]{0:T(128)S(1)}) all-reduce(f32[4]{0:T(128)S(1)} %dynamic-update-slice, f32[4]{0:T(128)S(1)} %convert_dynamic-update-slice_fusion), channel_id=1, replica_groups=mesh['groups'=2,'seq'=4,'beam'=4] {'beam'}, use_global_device_ids=true, to_apply=%add | all-reduce | flops 8 | bytes 64
  296.2 6.5 %all-reduce.10 = (f32[4]{0:T(128)S(1)}, f32[4]{0:T(128)S(1)}) all-reduce(f32[4]{0:T(128)S(1)} %dynamic-update-slice.2, f32[4]{0:T(128)S(1)} %dynamic-update-slice.3), channel_id=1, replica_groups=mesh['groups'=2,'seq'=4,'beam'=4] {'beam'}, use_global_device_ids=true, to_apply=%add.2 | all-reduce | flops 8 | bytes 64
  312.3 6.1 %all-reduce.9 = (f32[4]{0:T(128)S(1)}, f32[4]{0:T(128)S(1)}) all-reduce(f32[4]{0:T(128)S(1)} %dynamic-update-slice.4, f32[4]{0:T(128)S(1)} %dynamic-update-slice.5), channel_id=1, replica_groups=mesh['groups'=2,'seq'=4,'beam'=4] {'beam'}, use_global_device_ids=true, to_apply=%add.4 | all-reduce | flops 8 | bytes 64
  323.4 1.9 fusion.46
  328.1 6.1 %all-reduce.8 = (f32[4]{0:T(128)S(1)}, f32[4]{0:T(128)S(1)}) all-reduce(f32[4]{0:T(128)S(1)} %dynamic-update-slice.6, f32[4]{0:T(128)S(1)} %dynamic-update-slice.7), channel_id=1, replica_groups=mesh['groups'=2,'seq'=4,'beam'=4] {'beam'}, use_global_device_ids=true, to_apply=%add.6 | all-reduce | flops 8 | bytes 64
  339.4 7.0 %all-reduce.12 = (f32[1]{0:T(128)}, f32[1]{0:T(128)}, f32[1]{0:T(128)}, f32[1]{0:T(128)}) all-reduce(f32[1]{0:T(128)S(6)} %div.31, f32[1]{0:T(128)} %get-tuple-element.186, f32[1]{0:T(128)} %get-tuple-element.190, f32[1]{0:T(128)} %get-tuple-element.194), channel_id=1, replica_groups=mesh['groups'=2,'seq'=4,'beam'=4] {'beam'}, use_global_device_ids=true, to_apply=%region_19.20 | all-reduce | flops 4 | bytes 32 | tf_op jit(solution)/shard_map/pmax | solution.py:144
  353.9 3.7 fusion.7
  357.6 2.3 copy.54
  360.6 1.8 fusion.16
  362.5 1.8 fusion.17
  364.4 2.9 multiply_reduce_fusion
  (151 shorter events, 64.7 us)
Async XLA Ops:
  7.2 346.1 %copy-start = (bf16[256,128]{1,0:T(8,128)(2,1)S(1)}, bf16[256,128]{1,0:T(8,128)(2,1)}, u32[]{:S(2)}) copy-start(bf16[256,128]{1,0:T(8,128)(2,1)} %param.17) | copy-start | bytes 196612
  7.2 89.5 %all-gather.15.cloned.1.call-start = ((), (), s32[]{:S(2)}) async-start(), calls=%async_computation.3 | async-start | bytes 5242880 | tf_op jit(solution)/shard_map/all_gather | solution.py:70
  13.0 180.8 %all-gather.17.cloned.1.call-start = ((), (), s32[]{:S(2)}) async-start(), calls=%async_computation.4 | async-start | bytes 5242880 | tf_op jit(solution)/shard_map/all_gather | solution.py:115
  108.5 14.3 %collective-permute-start = (f32[32,64,128]{2,1,0:T(8,128)S(1)}, f32[32,64,128]{2,1,0:T(8,128)S(1)}, u32[]{:S(2)}, u32[]{:S(2)}) collective-permute-start(f32[32,64,128]{2,1,0:T(8,128)S(1)} %get-tuple-element.85), channel_id=1, source_target_pairs={{0,1},{1,2},{2,3},{3,0},{4,5},{5,6},{6,7},{7,4},{8,9},{9,10},{10,1... | collective-permute-start | bytes 3145736 | tf_op jit(solution)/shard_map/ppermute | solution.py:102
  122.7 1.0 copy-start.1
  123.7 14.3 %collective-permute-start.1 = (f32[32,64,128]{2,1,0:T(8,128)S(1)}, f32[32,64,128]{2,1,0:T(8,128)}, u32[]{:S(2)}, u32[]{:S(2)}) collective-permute-start(f32[32,64,128]{2,1,0:T(8,128)S(1)} %collective-permute-done), channel_id=1, source_target_pairs={{0,1},{1,2},{2,3},{3,0},{4,5},{5,6},{6,7},{7,4},{8,9},{9,10},{10,1... | collective-permute-start | bytes 3145736 | tf_op jit(solution)/shard_map/ppermute | solution.py:102
  138.0 14.5 %collective-permute-start.2 = (f32[32,64,128]{2,1,0:T(8,128)}, f32[32,64,128]{2,1,0:T(8,128)}, u32[]{:S(2)}, u32[]{:S(2)}) collective-permute-start(f32[32,64,128]{2,1,0:T(8,128)} %collective-permute-done.1), channel_id=1, source_target_pairs={{0,1},{1,2},{2,3},{3,0},{4,5},{5,6},{6,7},{7,4},{8,9},{9,10},{10,1... | collective-permute-start | bytes 3145736 | tf_op jit(solution)/shard_map/ppermute | solution.py:102
  138.0 21.4 %copy-start.2 = (f32[32,64,128]{2,1,0:T(8,128)S(1)}, f32[32,64,128]{2,1,0:T(8,128)}, u32[]{:S(2)}) copy-start(f32[32,64,128]{2,1,0:T(8,128)} %copy-done.1) | copy-start | bytes 3145732
  155.2 5.5 %copy-start.6 = (bf16[4,1,2048]{2,0,1:T(4,128)(2,1)S(1)}, bf16[4,1,2048]{2,0,1:T(4,128)(2,1)}, u32[]{:S(2)}) copy-start(bf16[4,1,2048]{2,0,1:T(4,128)(2,1)} %param.19) | copy-start | bytes 49156
  155.3 5.7 %copy-start.7 = (s32[4,1]{0,1:T(1,128)S(1)}, s32[4,1]{0,1:T(1,128)}, u32[]{:S(2)}) copy-start(s32[4,1]{0,1:T(1,128)} %param.25) | copy-start | bytes 52
  155.3 7.0 %copy-start.8 = (s32[4,1]{0,1:T(1,128)S(1)}, s32[4,1]{0,1:T(1,128)}, u32[]{:S(2)}) copy-start(s32[4,1]{0,1:T(1,128)} %param.24) | copy-start | bytes 52
  155.3 8.3 %copy-start.11 = (f32[4,1,32]{2,1,0:T(1,128)S(1)}, f32[4,1,32]{2,1,0:T(1,128)}, u32[]{:S(2)}) copy-start(f32[4,1,32]{2,1,0:T(1,128)} %param.22) | copy-start | bytes 1540
  155.3 8.3 %copy-start.10 = (bf16[4,1,128]{2,0,1:T(4,128)(2,1)S(1)}, bf16[4,1,128]{2,0,1:T(4,128)(2,1)}, u32[]{:S(2)}) copy-start(bf16[4,1,128]{2,0,1:T(4,128)(2,1)} %param.20) | copy-start | bytes 3076
  160.7 72.0 %all-gather.9.cloned.1.call-start = ((), (), s32[]{:S(2)}) async-start(), calls=%async_computation | async-start | bytes 5242880 | tf_op jit(solution)/shard_map/all_gather | solution.py:115
  198.1 74.5 %all-gather.11.cloned.1.call-start = ((), (), s32[]{:S(2)}) async-start(), calls=%async_computation.1 | async-start | bytes 5242880 | tf_op jit(solution)/shard_map/all_gather | solution.py:115
  199.5 79.7 %copy-start.13 = (u32[32]{0:T(128)S(1)}, u32[32]{0:T(128)}, u32[]{:S(2)}) copy-start(u32[32]{0:T(128)} %constant.142) | copy-start | bytes 388
  199.5 91.5 %copy-start.9 = (f32[4,1]{0,1:T(1,128)S(1)}, f32[4,1]{0,1:T(1,128)}, u32[]{:S(2)}) copy-start(f32[4,1]{0,1:T(1,128)} %param.23) | copy-start | bytes 52
  199.5 153.7 %copy-start.5 = (bf16[256,128]{1,0:T(8,128)(2,1)S(1)}, bf16[256,128]{1,0:T(8,128)(2,1)}, u32[]{:S(2)}) copy-start(bf16[256,128]{1,0:T(8,128)(2,1)} %param.16) | copy-start | bytes 196612
  235.6 1.0 copy-start.3
  237.9 126.5 %all-gather.13.cloned.1.call-start = ((), (), s32[]{:S(2)}) async-start(), calls=%async_computation.2 | async-start | bytes 5242880 | tf_op jit(solution)/shard_map/all_gather | solution.py:115
  275.4 1.0 copy-start.4
  353.9 6.0 %copy-start.12 = (bf16[4,1,128]{2,0,1:T(4,128)(2,1)S(1)}, bf16[4,1,128]{2,0,1:T(4,128)(2,1)}, u32[]{:S(2)}) copy-start(bf16[4,1,128]{2,0,1:T(4,128)(2,1)} %param.21) | copy-start | bytes 3076
Sparse Core Ops, SparseCore 0:
  13.2 83.4 all-gather.14
  160.9 32.9 all-gather.16
  198.2 34.4 all-gather.8
  238.1 34.4 all-gather.10
  278.0 34.5 all-gather.12
